TPU v7x, 32 devices: a whole 2x2x4 slice. The times are simulated.
32 devices in a mesh: groups: 2 (over x), seq: 16 (over z, y, core).
Axes of the slice: x: 2, y: 2, z: 4, core: 2. Of those that a mesh axis runs over, the one named last changes fastest.
Arguments:
- hidden: bfloat16 [1024, 3072], P(('groups', 'seq')), parts along dimension 0, may hold values from -6 to 6
- queries: bfloat16 [1024, 3072], P(('groups', 'seq')), parts along dimension 0, may hold values from -6 to 6
- key_rows: bfloat16 [1024, 3072], P(('groups', 'seq')), parts along dimension 0, may hold values from -6 to 6
- values: bfloat16 [1024, 3072], P(('groups', 'seq')), parts along dimension 0, may hold values from -12 to 12
- query_gain: float32 [2, 128], replicated, may hold values from 0.6 to 5
- key_gain: float32 [2, 128], replicated, may hold values from 0.6 to 5
- gate_table: bfloat16 [8, 2, 3072], P('groups'), parts along dimension 0, may hold values from -6 to 6
- segment: int32 [1024], P(('groups', 'seq')), parts along dimension 0, may hold values from 0 to 3, as said below
- text_count: int32 [8], P('groups'), parts along dimension 0, may hold values from 1 to 40
Outputs:
- mixed: bfloat16 [1024, 3072], P(('groups', 'seq')), parts along dimension 0
There are 2 independent parts, one for each index of `groups`. A program takes and returns all parts, laid end to end along the dimension named above; an argument that names none is the same for every part. Nothing has to cross between parts.
Inputs may be any that keep to these rules, and one draw needn't show every extreme that they name: `segment`: one device holds at most 10 tokens of one request; in every draw some two requests 2 j and 2 j + 1 get exactly 10 tokens from every device. Tokens of one request may lie anywhere on the devices.
All inputs are finite; a program needn't handle non-finite values.
Results may differ from a plain program's by a relative error of at most 0.012.
The roundings to bfloat16 on the way count: a program that leaves them out, or rounds other values in their place, can miss the bound.
Values may be sent and summed in bfloat16 or wider, within the bound.
A program may use at most 64 MiB of HBM per device.

v0:
```python
import math

import jax
import jax.numpy as jnp
from jax import lax
from jax.sharding import PartitionSpec as P

HEAD_DIM = 128


EPSILON = 1e-06
MASKED = -1e30


def head_norm(rows_in, gains, stream):
    row_count = rows_in.shape[0]
    per_head = rows_in.astype(jnp.float32).reshape(row_count, -1, HEAD_DIM)
    inverse = lax.rsqrt(jnp.mean(per_head * per_head, axis=-1, keepdims=True) + EPSILON)
    gain_rows = jnp.where((stream == 0)[:, None], gains[0][None, :], gains[1][None, :])
    return (per_head * inverse * gain_rows[:, None, :]).astype(jnp.bfloat16).reshape(row_count, -1)


def attend(query_block, block_segment, key_data, value_data, key_segment):
    scores = jnp.einsum(
        "qhd,khd->hqk", query_block, key_data, preferred_element_type=jnp.float32
    ) * (1.0 / math.sqrt(HEAD_DIM))
    allowed = (block_segment[:, None] == key_segment[None, :])[None, :, :]
    scores = jnp.where(allowed, scores, MASKED)
    largest = jnp.max(scores, axis=-1, keepdims=True)
    weights = jnp.exp(scores - largest)
    weights = (weights / jnp.sum(weights, axis=-1, keepdims=True)).astype(jnp.bfloat16)
    return jnp.einsum(
        "hqk,khd->qhd", weights, value_data, preferred_element_type=jnp.float32
    ).astype(jnp.bfloat16)


def per_device(
    hidden, queries, key_rows, values, query_gain, key_gain, gate_table, segment, text_count
):
    tok_rows = hidden.shape[0]
    width_all = hidden.shape[1]
    devices = lax.axis_size("seq")
    requests = text_count.shape[0]
    seg_hot = (segment[:, None] == jnp.arange(requests, dtype=jnp.int32)[None, :]).astype(jnp.int32)
    local_counts = jnp.sum(seg_hot, axis=0)
    all_counts = lax.all_gather(local_counts[None, :], "seq", axis=0, tiled=True)
    lower_rows = (jnp.arange(devices, dtype=jnp.int32) < lax.axis_index("seq")).astype(jnp.int32)
    before = jnp.sum(all_counts * lower_rows[:, None], axis=0)
    position = jnp.sum((jnp.cumsum(seg_hot, axis=0) - seg_hot + before[None, :]) * seg_hot, axis=1)
    text_limit = jnp.sum(seg_hot * text_count[None, :], axis=1)
    stream = (position >= text_limit).astype(jnp.int32)
    query_normed = head_norm(queries, query_gain, stream)
    key_normed = head_norm(key_rows, key_gain, stream)
    groups = 8
    pair_merge = 2
    slices = devices // groups
    cap_rows = 4 * tok_rows // devices + max(1, tok_rows // devices)
    bucket_rows = cap_rows * pair_merge
    head_cols = width_all // groups
    owner_slice = segment // pair_merge
    owner_hot = (owner_slice[:, None] == jnp.arange(slices, dtype=jnp.int32)[None, :]).astype(
        jnp.int32
    )
    owner_rank = jnp.sum((jnp.cumsum(owner_hot, axis=0) - owner_hot) * owner_hot, axis=1)
    slot_place = owner_slice * bucket_rows + owner_rank
    bucket_index = (
        jnp.full((slices * bucket_rows,), tok_rows, jnp.int32)
        .at[slot_place]
        .set(jnp.arange(tok_rows, dtype=jnp.int32))
    )
    stacked = jnp.concatenate(
        [
            query_normed.reshape(tok_rows, groups, head_cols),
            key_normed.reshape(tok_rows, groups, head_cols),
            values.reshape(tok_rows, groups, head_cols),
        ],
        axis=2,
    ).transpose(1, 0, 2)
    outgoing = jnp.take(stacked, bucket_index, axis=1, mode="fill", fill_value=0).reshape(
        devices, bucket_rows, 3 * head_cols
    )
    slot_segment = jnp.take(segment, bucket_index, axis=0, mode="fill", fill_value=-1)
    segment_out = jnp.broadcast_to(slot_segment[None, :], (groups, slices * bucket_rows)).reshape(
        devices, bucket_rows
    )
    arrived, arrived_segment = (
        lax.all_to_all(outgoing, "seq", split_axis=0, concat_axis=0, tiled=True),
        lax.all_to_all(segment_out, "seq", split_axis=0, concat_axis=0, tiled=True),
    )
    slot_count = devices * bucket_rows
    per_head = head_cols // HEAD_DIM
    slot_data = arrived.reshape(slot_count, 3 * head_cols)
    query_all = slot_data[:, :head_cols].reshape(slot_count, per_head, HEAD_DIM)
    key_all = slot_data[:, head_cols : 2 * head_cols].reshape(slot_count, per_head, HEAD_DIM)
    value_all = slot_data[:, 2 * head_cols :].reshape(slot_count, per_head, HEAD_DIM)
    key_segment = arrived_segment.reshape(slot_count)
    if slot_count % 512 == 0:
        block_rows = 512
    elif slot_count % 256 == 0:
        block_rows = 256
    else:
        block_rows = slot_count

    def one_block(first_row):
        return attend(query_all, key_segment, key_all, value_all, key_segment)

    results = lax.map(one_block, jnp.arange(slot_count // block_rows, dtype=jnp.int32) * block_rows)
    returning = results.reshape(devices, bucket_rows, head_cols)
    returned = lax.all_to_all(returning, "seq", split_axis=0, concat_axis=0, tiled=True)
    returned = returned.reshape(groups, slices * bucket_rows, head_cols)
    attention = (
        jnp.take(returned, slot_place, axis=1).transpose(1, 0, 2).reshape(tok_rows, width_all)
    )
    gate_rows = jnp.take(gate_table.reshape(requests * 2, width_all), segment * 2 + stream, axis=0)
    mixed = hidden.astype(jnp.float32) + gate_rows.astype(jnp.float32) * attention.astype(
        jnp.float32
    )
    return mixed.astype(jnp.bfloat16)


def solution(mesh):
    return jax.shard_map(
        per_device,
        mesh=mesh,
        in_specs=(
            P(("groups", "seq"), None),
            P(("groups", "seq"), None),
            P(("groups", "seq"), None),
            P(("groups", "seq"), None),
            P(),
            P(),
            P("groups", None, None),
            P(("groups", "seq")),
            P("groups"),
        ),
        out_specs=P(("groups", "seq"), None),
        check_vma=False,
    )
```

profile of v0, /device:TPU:0, one launch (start us, length us, event | category | flops | bytes accessed | tf_op | source)
XLA Modules:
  0.0 80.8 jit_solution(14625927851329295518)
XLA Ops:
  0.0 0.7 and_select_fusion
  0.7 0.1 fusion.8
  0.8 0.1 reduce_window_sum.23
  0.8 0.2 select_reduce_fusion
  1.0 0.7 compare_and_fusion.1
  1.7 0.7 scatter_custom_fusion
  2.4 1.4 %gather_fusion.2 = s32[40]{0:T(128)S(1)} fusion(s32[32]{0:T(128)} %param.16, s32[1024]{0:T(1024)S(1)} %pad_clamp_fusion.1), kind=kCustom, calls=%fused_computation.2 | custom fusion | bytes 480 | tf_op jit(solution)/shard_map/jit(_take)/gather | solution.py:82
  3.9 0.1 broadcast_in_dim.170
  3.9 0.6 broadcast_in_dim.171
  4.5 7.4 %all-to-all-start.1 = ((s32[16,1,20]{2,1,0:T(1,128)}), s32[16,1,20]{2,1,0:T(1,128)S(1)}, u32[]{:S(2)}, u32[]{:S(2)}) async-start(s32[16,1,20]{2,1,0:T(1,128)} %bitcast.8), calls=%async_computation.1 | async-start | bytes 16384 | tf_op jit(solution)/shard_map/all_to_all | solution.py:88
  12.0 0.7 fusion.9
  12.7 0.9 %select_reduce_fusion.1 = (s32[32]{0:T(128)S(1)}, s32[4]{0:T(128)S(1)}) fusion(s32[4]{0:T(128)} %param.17, s32[32]{0:T(128)} %param.16), kind=kLoop, calls=%fused_computation.30 | loop fusion | flops 604 | bytes 288 | tf_op jit(solution)/shard_map/reduce_sum | solution.py:50
  13.6 1.3 %dynamic-slice = u32[1]{0:T(128)} dynamic-slice(u32[32]{0:T(128)} %constant.119, u32[]{:T(128)S(6)} %add.76), dynamic_slice_sizes={1} | dynamic-slice | bytes 12
  15.6 0.2 dynamic-update-slice
  15.8 12.4 %all-reduce = s32[64]{0:T(128)S(1)} all-reduce(s32[64]{0:T(128)S(1)} %dynamic-update-slice), channel_id=2, replica_groups=mesh['groups'=2,'seq'=16] {'seq'}, use_global_device_ids=true, to_apply=%add | all-reduce | flops 64 | bytes 512
  28.2 0.1 reshape.267
  28.3 0.1 reduce_window_sum.22
  28.4 0.1 multiply_reduce_fusion
  28.5 0.8 %select_reduce_fusion.2 = s32[32]{0:T(128)S(1)} fusion(s32[32,4]{1,0:T(8,128)S(1)} %reduce_window_sum.22, s32[4]{0:T(128)S(1)} %multiply_reduce_fusion, s32[32]{0:T(128)} %param.16), kind=kLoop, calls=%fused_computation.31 | loop fusion | flops 736 | bytes 784 | tf_op jit(solution)/shard_map/reduce_sum | solution.py:49
  29.3 0.7 compare_and_fusion.2
  30.0 0.8 slice_bitcast_fusion.1
  30.7 0.1 broadcast_select_fusion.2
  30.8 0.1 mul.121
  31.0 0.1 copy.47
  31.1 0.2 reduce_sum.79
  31.3 0.2 mul.117
  31.4 0.1 mul.118
  31.6 0.1 mul.113
  31.7 0.5 copy-done.1
  32.2 0.1 copy.45
  32.3 0.2 reduce_sum.78
  32.5 0.2 mul.109
  32.7 0.1 mul.110
  32.8 0.3 copy-done.3
  33.2 0.1 fusion.5
  33.3 0.1 fusion.7
  33.3 0.1 maximum_bitcast_fusion
  33.4 0.7 gather_fusion.1
  34.1 0.1 copy.30
  34.2 0.1 gather.20
  34.3 0.1 broadcast_in_dim.154
  34.4 1.1 %broadcast_select_fusion = bf16[16,20,1152]{2,1,0:T(8,128)(2,1)} fusion(bf16[16,20,1152]{2,1,0:T(8,128)(2,1)S(1)} %gather.20, pred[16,20]{1,0:T(8,128)(4,1)S(1)} %broadcast_in_dim.156), kind=kLoop, calls=%fused_computation.12 | loop fusion | flops 368640 | bytes 1474880 | tf_op jit(solution)/shard_map/jit(_take)/select_n | solution.py:79
  35.5 3.6 %all-to-all-start = ((bf16[16,20,1152]{2,1,0:T(8,128)(2,1)}), bf16[16,20,1152]{2,1,0:T(8,128)(2,1)S(1)}, u32[]{:S(2)}, u32[]{:S(2)}) async-start(bf16[16,20,1152]{2,1,0:T(8,128)(2,1)} %broadcast_select_fusion), calls=%async_computation | async-start | bytes 1769472 | tf_op jit(solution)/shard_map/all_to_all | solution.py:87
  39.2 0.5 broadcast.184
  39.7 0.7 reduce.3
  40.4 0.1 eq.67
  40.4 0.1 broadcast_compare_fusion
  40.6 18.8 %all-to-all-done = bf16[16,20,1152]{2,1,0:T(8,128)(2,1)S(1)} async-done(((bf16[16,20,1152]{2,1,0:T(8,128)(2,1)}), bf16[16,20,1152]{2,1,0:T(8,128)(2,1)S(1)}, u32[]{:S(2)}, u32[]{:S(2)}) %all-to-all-start) | async-done | bytes 737312 | tf_op jit(solution)/shard_map/all_to_all | solution.py:87
  59.4 0.1 reshape.220
  59.5 0.1 fusion.16
  59.6 0.2 copy.33
  59.8 0.2 copy.32
  60.1 0.2 copy.31
  60.3 0.7 fusion.17
  61.0 0.5 fusion.3
  61.5 0.2 copy.38
  61.7 0.9 %reshape.224 = bf16[16,20,384]{2,1,0:T(8,128)(2,1)} reshape(bf16[320,3,128]{2,1,0:T(4,128)(2,1)S(1)} %copy.38) | data formatting | bytes 491520 | tf_op jit(solution)/shard_map/reshape | solution.py:108
  62.7 5.9 %all-to-all-start.2 = ((bf16[16,20,384]{2,1,0:T(8,128)(2,1)}), bf16[16,20,384]{2,1,0:T(8,128)(2,1)S(1)}, u32[]{:S(2)}, u32[]{:S(2)}) async-start(bf16[16,20,384]{2,1,0:T(8,128)(2,1)} %reshape.224), calls=%async_computation.2 | async-start | bytes 589824 | tf_op jit(solution)/shard_map/all_to_all | solution.py:109
  68.6 0.7 gather_fusion
  69.3 9.8 %all-to-all-done.2 = bf16[16,20,384]{2,1,0:T(8,128)(2,1)S(1)} async-done(((bf16[16,20,384]{2,1,0:T(8,128)(2,1)}), bf16[16,20,384]{2,1,0:T(8,128)(2,1)S(1)}, u32[]{:S(2)}, u32[]{:S(2)}) %all-to-all-start.2) | async-done | bytes 245792 | tf_op jit(solution)/shard_map/all_to_all | solution.py:109
  79.2 0.6 gather_fusion.3
  79.8 0.1 select_convert_fusion
  79.9 0.1 copy.49
  80.0 0.8 %add_convert_fusion = bf16[32,3072]{1,0:T(8,128)(2,1)} fusion(f32[32,3072]{1,0:T(8,128)S(1)} %bitcast.48, bf16[32,3072]{1,0:T(8,128)(2,1)S(1)} %copy-done.2, bf16[32,3072]{1,0:T(8,128)(2,1)S(1)} %gather_fusion, pred[32]{0:T(512)(128)(4,1)S(1)} %get-tuple-element.17), kind=kLoop, calls=%fused_computation.20 | loop fusion | flops 589824 | bytes 983072 | tf_op jit(solution)/shard_map/convert_element_type | solution.py:118
  (31 shorter events, 0.4 us)
Async XLA Ops:
  0.0 30.9 %copy-start = (bf16[32,3072]{1,0:T(8,128)(2,1)S(1)}, bf16[32,3072]{1,0:T(8,128)(2,1)}, u32[]{:S(2)}) copy-start(bf16[32,3072]{1,0:T(8,128)(2,1)} %param.11) | copy-start | bytes 589828
  4.5 31.0 %all-to-all-start.1 = ((s32[16,1,20]{2,1,0:T(1,128)}), s32[16,1,20]{2,1,0:T(1,128)S(1)}, u32[]{:S(2)}, u32[]{:S(2)}) async-start(s32[16,1,20]{2,1,0:T(1,128)} %bitcast.8), calls=%async_computation.1 | async-start | bytes 16384 | tf_op jit(solution)/shard_map/all_to_all | solution.py:88
  31.3 0.9 %copy-start.1 = (bf16[32,3072]{1,0:T(8,128)(2,1)S(1)}, bf16[32,3072]{1,0:T(8,128)(2,1)}, u32[]{:S(2)}) copy-start(bf16[32,3072]{1,0:T(8,128)(2,1)} %param.10) | copy-start | bytes 589828
  32.2 0.9 %copy-start.3 = (bf16[32,3072]{1,0:T(8,128)(2,1)S(1)}, bf16[32,3072]{1,0:T(8,128)(2,1)}, u32[]{:S(2)}) copy-start(bf16[32,3072]{1,0:T(8,128)(2,1)} %param.12) | copy-start | bytes 589828
  35.5 23.9 %all-to-all-start = ((bf16[16,20,1152]{2,1,0:T(8,128)(2,1)}), bf16[16,20,1152]{2,1,0:T(8,128)(2,1)S(1)}, u32[]{:S(2)}, u32[]{:S(2)}) async-start(bf16[16,20,1152]{2,1,0:T(8,128)(2,1)} %broadcast_select_fusion), calls=%async_computation | async-start | bytes 1769472 | tf_op jit(solution)/shard_map/all_to_all | solution.py:87
  61.5 7.0 %copy-start.4 = (bf16[4,2,3072]{2,1,0:T(2,128)(2,1)S(1)}, bf16[4,2,3072]{2,1,0:T(2,128)(2,1)}, u32[]{:S(2)}) copy-start(bf16[4,2,3072]{2,1,0:T(2,128)(2,1)} %param.15) | copy-start | bytes 147460
  62.7 16.4 %all-to-all-start.2 = ((bf16[16,20,384]{2,1,0:T(8,128)(2,1)}), bf16[16,20,384]{2,1,0:T(8,128)(2,1)S(1)}, u32[]{:S(2)}, u32[]{:S(2)}) async-start(bf16[16,20,384]{2,1,0:T(8,128)(2,1)} %reshape.224), calls=%async_computation.2 | async-start | bytes 589824 | tf_op jit(solution)/shard_map/all_to_all | solution.py:109
  69.3 10.7 %copy-start.2 = (bf16[32,3072]{1,0:T(8,128)(2,1)S(1)}, bf16[32,3072]{1,0:T(8,128)(2,1)}, u32[]{:S(2)}) copy-start(bf16[32,3072]{1,0:T(8,128)(2,1)} %param.9) | copy-start | bytes 589828
where the time goes:
time: 81.3 us; the launch traced here: 80.8 us
  waiting for transfers between devices  28.6 us (35%)
  starting transfers between devices  16.9 us (21%)
  blocking collectives  12.4 us (15%)
  local copies, waits for them, and re-layouts  12.1 us (15%)
  other arithmetic  8.49 us (10%)
  matrix products  1.2 us (1%)
  between operations  1.12 us (1%)
    all_to_all x1, waiting for transfers between devices, per_device(): lax.all_to_all(outgoing, 'seq', split_axis=0, concat_axis=0, tiled=True)  18.8 us
    unnamed x1, blocking collectives  12.4 us
    all_to_all x1, waiting for transfers between devices, per_device(): lax.all_to_all(returning, 'seq', split_axis=0, concat_axis=0, tiled=True)  9.79 us
    all_to_all x1, starting transfers between devices, per_device(): lax.all_to_all(segment_out, 'seq', split_axis=0, concat_axis=0, tiled=True)  7.41 us
    all_to_all x1, starting transfers between devices, per_device(): lax.all_to_all(returning, 'seq', split_axis=0, concat_axis=0, tiled=True)  5.86 us
    all_to_all x1, starting transfers between devices, per_device(): lax.all_to_all(outgoing, 'seq', split_axis=0, concat_axis=0, tiled=True)  3.63 us
    unnamed x19, local copies, waits for them, and re-layouts  2.71 us
  transfers between devices with their start and end apart: 3, of which 2 were waited for; matrix products, arithmetic and copies ran while one was open for 14% of the time, Pallas kernels for 0%

commit v1 on v0

--- a/solution.py
+++ b/solution.py
@@ -1,8 +1,11 @@
+import functools
 import math
 
 import jax
 import jax.numpy as jnp
 from jax import lax
+from jax.experimental import pallas as pl
+from jax.experimental.pallas import tpu as pltpu
 from jax.sharding import PartitionSpec as P
 
 HEAD_DIM = 128
@@ -118,9 +121,279 @@
     return mixed.astype(jnp.bfloat16)
 
 
+LANES = 128
+CONTRACT_LAST = (((1,), (1,)), ((), ()))
+
+
+def normed(rows, gain_rows):
+    wide = rows.astype(jnp.float32)
+    inverse = lax.rsqrt(jnp.mean(wide * wide, axis=-1, keepdims=True) + EPSILON)
+    return (wide * inverse * gain_rows).astype(jnp.bfloat16)
+
+
+def fused_kernel(
+    devices, requests, text_ref, segment_ref, hidden_ref, query_hbm, key_hbm, value_hbm,
+    query_gain_ref, key_gain_ref, gate_ref, out_ref,
+    stage, recv, query_n, key_n, result, back, seg_all, hot, text, bias, gate_rows,
+    stage_sem, own_sem, seg_own_sem, seg_send, seg_recv,
+    out_send, out_recv, relay_send, relay_recv, back_send, back_recv,
+):
+    chips = devices // 2
+    tok = hidden_ref.shape[0]
+    per_chip = hidden_ref.shape[1] // HEAD_DIM // chips
+    tokens = devices * tok
+    mine = chips * tok
+    me = lax.axis_index("seq")
+    chip, core = me // 2, me % 2
+    partner = me + 1 - 2 * core
+    sources = (query_hbm, key_hbm, value_hbm)
+
+    def columns(head):
+        return pl.ds(pl.multiple_of(head * HEAD_DIM, HEAD_DIM), HEAD_DIM)
+
+    def remote(src, dst, send_sem, recv_sem, device):
+        return pltpu.make_async_remote_copy(
+            src_ref=src, dst_ref=dst, send_sem=send_sem, recv_sem=recv_sem,
+            device_id={"seq": device}, device_id_type=pl.DeviceIdType.MESH,
+        )
+
+    barrier = pltpu.get_barrier_semaphore()
+    for step in range(1, devices):
+        pl.semaphore_signal(
+            barrier, inc=1, device_id={"seq": (me + step) % devices},
+            device_id_type=pl.DeviceIdType.MESH,
+        )
+    for head in range(per_chip):
+        for step in range(1, chips):
+            target = (chip + step) % chips
+            for part, source in enumerate(sources):
+                pltpu.make_async_copy(
+                    source.at[:, columns(target * per_chip + head)],
+                    stage.at[head, step - 1, part],
+                    stage_sem.at[head],
+                ).start()
+        for part, source in enumerate(sources):
+            pltpu.make_async_copy(
+                source.at[:, columns(chip * per_chip + head)],
+                recv.at[head, me, part],
+                own_sem.at[head],
+            ).start()
+    seg_own = pltpu.make_async_copy(segment_ref, seg_all.at[me], seg_own_sem)
+    seg_own.start()
+    pl.semaphore_wait(barrier, devices - 1)
+
+    seg_copies = []
+    for step in range(1, devices):
+        copy = remote(
+            segment_ref, seg_all.at[me], seg_send.at[step - 1], seg_recv.at[step - 1],
+            (me + step) % devices,
+        )
+        copy.start()
+        seg_copies.append(copy)
+    out_copies = []
+    for head in range(per_chip):
+        pltpu.make_async_copy(stage.at[head], stage.at[head], stage_sem.at[head]).wait()
+        row = []
+        for step in range(1, chips):
+            copy = remote(
+                stage.at[head, step - 1], recv.at[head, me],
+                out_send.at[head, step - 1], out_recv.at[head, step - 1],
+                (chip + step) % chips * 2 + core,
+            )
+            copy.start()
+            row.append(copy)
+        out_copies.append(row)
+
+    relay_copies = []
+
+    def relay(head, step, source):
+        copy = remote(
+            recv.at[head, source, pl.ds(1, 2)], recv.at[head, source, pl.ds(1, 2)],
+            relay_send.at[head, step], relay_recv.at[head, step], partner,
+        )
+        copy.start()
+        return copy
+
+    for head in range(per_chip):
+        pltpu.make_async_copy(
+            recv.at[head, me], recv.at[head, me], own_sem.at[head]
+        ).wait()
+        relay_copies.append([relay(head, 0, me)])
+
+    seg_own.wait()
+    for copy in seg_copies:
+        copy.wait_recv()
+    eye = (
+        lax.broadcasted_iota(jnp.int32, (tok, tok), 0)
+        == lax.broadcasted_iota(jnp.int32, (tok, tok), 1)
+    ).astype(jnp.float32).astype(jnp.bfloat16)
+    ids = lax.broadcasted_iota(jnp.int32, (LANES, tok), 0)
+    for n in range(devices):
+        flipped = (ids == seg_all[n]).astype(jnp.float32).astype(jnp.bfloat16)
+        hot[n] = lax.dot_general(
+            eye, flipped, CONTRACT_LAST, preferred_element_type=jnp.float32
+        ).astype(jnp.bfloat16)
+    all_hot = hot[...].reshape(tokens, LANES)
+    earlier = (
+        lax.broadcasted_iota(jnp.int32, (tokens, tokens), 1)
+        < lax.broadcasted_iota(jnp.int32, (tokens, tokens), 0)
+    ).astype(jnp.float32).astype(jnp.bfloat16)
+    before = jnp.dot(earlier, all_hot, preferred_element_type=jnp.float32)
+    lane = lax.broadcasted_iota(jnp.int32, (1, LANES), 1)
+    limit = jnp.zeros((1, LANES), jnp.int32)
+    for r in range(requests):
+        limit = jnp.where(lane == r, text_ref[r], limit)
+    inside = jnp.where(before < limit.astype(jnp.float32), all_hot.astype(jnp.float32), 0.0)
+    ones = jnp.ones((LANES, LANES), jnp.bfloat16)
+    text[...] = jnp.dot(
+        inside.astype(jnp.bfloat16), ones, preferred_element_type=jnp.float32
+    ).reshape(devices, tok, LANES)
+    for c in range(chips):
+        same = lax.dot_general(
+            hot[2 * c + core], all_hot, CONTRACT_LAST, preferred_element_type=jnp.float32
+        )
+        bias[c * tok : (c + 1) * tok] = jnp.where(same > 0.5, 0.0, MASKED)
+
+    number = lax.broadcasted_iota(jnp.int32, (LANES, LANES), 0).astype(jnp.float32)
+    own_id = jnp.dot(
+        hot[me], number.astype(jnp.bfloat16), preferred_element_type=jnp.float32
+    )
+    own_code = 2.0 * own_id + jnp.where(text[me] > 0.5, 0.0, 1.0)
+    for tile in range(hidden_ref.shape[1] // LANES):
+        cols = slice(tile * LANES, (tile + 1) * LANES)
+        total = jnp.zeros((tok, LANES), jnp.float32)
+        for r in range(requests):
+            pair = gate_ref[r, :, cols].astype(jnp.float32)
+            for s in range(2):
+                total = jnp.where(own_code == float(2 * r + s), pair[s : s + 1], total)
+        gate_rows[tile] = total
+
+    query_gain, key_gain = query_gain_ref[...], key_gain_ref[...]
+
+    def gain_of(gain, n):
+        return jnp.where(text[n] > 0.5, gain[0:1], gain[1:2])
+
+    scale = 1.0 / math.sqrt(HEAD_DIM)
+    back_copies = []
+    for head in range(per_chip):
+        for step in range(1, chips):
+            out_copies[head][step - 1].wait_recv()
+            source = (chip + chips - step) % chips * 2 + core
+            relay_copies[head].append(relay(head, step, source))
+        for c in range(chips):
+            n = 2 * c + core
+            query_n[c] = normed(recv[head, n, 0], gain_of(query_gain, n))
+            key_n[n] = normed(recv[head, n, 1], gain_of(key_gain, n))
+        for step in range(chips):
+            relay_copies[head][step].wait_recv()
+            n = (chip + chips - step) % chips * 2 + 1 - core
+            key_n[n] = normed(recv[head, n, 1], gain_of(key_gain, n))
+        keys = key_n[...].reshape(tokens, HEAD_DIM)
+        vals = recv[head, :, 2].reshape(tokens, HEAD_DIM)
+        scores = lax.dot_general(
+            query_n[...].reshape(mine, HEAD_DIM), keys, CONTRACT_LAST,
+            preferred_element_type=jnp.float32,
+        ) * scale + bias[...]
+        largest = jnp.max(scores, axis=-1, keepdims=True)
+        weights = jnp.exp(scores - largest)
+        weights = (weights / jnp.sum(weights, axis=-1, keepdims=True)).astype(jnp.bfloat16)
+        result[head] = jnp.dot(
+            weights, vals, preferred_element_type=jnp.float32
+        ).astype(jnp.bfloat16).reshape(chips, tok, HEAD_DIM)
+        row = []
+        for step in range(1, chips):
+            target = (chip + step) % chips
+            copy = remote(
+                result.at[head, target], back.at[chip * per_chip + head],
+                back_send.at[head, step - 1], back_recv.at[head, step - 1],
+                target * 2 + core,
+            )
+            copy.start()
+            row.append(copy)
+        back_copies.append(row)
+
+    def finish(index, attention):
+        out_ref[:, columns(index)] = (
+            hidden_ref[:, columns(index)].astype(jnp.float32)
+            + gate_rows[index] * attention.astype(jnp.float32)
+        ).astype(jnp.bfloat16)
+
+    for head in range(per_chip):
+        finish(chip * per_chip + head, result[head, chip])
+        for step in range(1, chips):
+            back_copies[head][step - 1].wait_recv()
+            index = (chip + chips - step) % chips * per_chip + head
+            finish(index, back[index])
+    for copy in seg_copies:
+        copy.wait_send()
+    for rows in (out_copies, relay_copies, back_copies):
+        for row in rows:
+            for copy in row:
+                copy.wait_send()
+
+
+def fused(
+    hidden, queries, key_rows, values, query_gain, key_gain, gate_table, segment, text_count
+):
+    devices = lax.axis_size("seq")
+    chips = devices // 2
+    tok, width = hidden.shape
+    heads = width // HEAD_DIM
+    per_chip = heads // chips
+    vmem = pl.BlockSpec(memory_space=pltpu.VMEM)
+    hbm = pl.BlockSpec(memory_space=pl.ANY)
+    block = (tok, HEAD_DIM)
+    dma = pltpu.SemaphoreType.DMA
+    return pl.pallas_call(
+        functools.partial(fused_kernel, devices, text_count.shape[0]),
+        out_shape=jax.ShapeDtypeStruct((tok, width), jnp.bfloat16),
+        in_specs=[pl.BlockSpec(memory_space=pltpu.SMEM), vmem, vmem, hbm, hbm, hbm]
+        + [vmem] * 3,
+        out_specs=vmem,
+        scratch_shapes=[
+            pltpu.VMEM((per_chip, chips - 1, 3) + block, jnp.bfloat16),
+            pltpu.VMEM((per_chip, devices, 3) + block, jnp.bfloat16),
+            pltpu.VMEM((chips,) + block, jnp.bfloat16),
+            pltpu.VMEM((devices,) + block, jnp.bfloat16),
+            pltpu.VMEM((per_chip, chips) + block, jnp.bfloat16),
+            pltpu.VMEM((heads,) + block, jnp.bfloat16),
+            pltpu.VMEM((devices, 1, tok), jnp.int32),
+            pltpu.VMEM((devices, tok, LANES), jnp.bfloat16),
+            pltpu.VMEM((devices, tok, LANES), jnp.float32),
+            pltpu.VMEM((chips * tok, devices * tok), jnp.float32),
+            pltpu.VMEM((heads, tok, LANES), jnp.float32),
+            dma((per_chip,)),
+            dma((per_chip,)),
+            dma,
+            dma((devices - 1,)),
+            dma((devices - 1,)),
+            dma((per_chip, chips - 1)),
+            dma((per_chip, chips - 1)),
+            dma((per_chip, chips)),
+            dma((per_chip, chips)),
+            dma((per_chip, chips - 1)),
+            dma((per_chip, chips - 1)),
+        ],
+        compiler_params=pltpu.CompilerParams(collective_id=0, has_side_effects=True),
+    )(
+        text_count, segment.reshape(1, tok), hidden, queries, key_rows, values,
+        query_gain, key_gain, gate_table,
+    )
+
+
+def program(*arrays):
+    devices = lax.axis_size("seq")
+    tok, width = arrays[0].shape
+    requests = arrays[-1].shape[0]
+    whole_heads = devices % 2 == 0 and (width // HEAD_DIM) % (devices // 2) == 0
+    if whole_heads and devices * tok <= 1024 and requests <= LANES and tok % 16 == 0:
+        return fused(*arrays)
+    return per_device(*arrays)
+
+
 def solution(mesh):
     return jax.shard_map(
-        per_device,
+        program,
         mesh=mesh,
         in_specs=(
             P(("groups", "seq"), None),

time: 81.3 us -> 33.6 us (0.41)
  Pallas kernels: 0 us -> 31.8 us
  waiting for transfers between devices: 28.6 us -> 0 us
  starting transfers between devices: 16.9 us -> 0 us
  blocking collectives: 12.4 us -> 0 us
  local copies, waits for them, and re-layouts: 12.1 us -> 1.62 us
  other arithmetic: 8.49 us -> 0 us
  matrix products: 1.2 us -> 0 us
  between operations: 1.12 us -> 0.01 us
    pallas_call x0 -> x1, Pallas kernels: none -> 31.8 us  [fused(): pl.pallas_call(functools.partial(fused_kernel, devices, text_count.shape[...]
    all_to_all x3 -> x0, waiting for transfers between devices: 28.6 us -> none  [the longest x1 18.8 us: per_device(): lax.all_to_all(outgoing, 'seq', split_axis=0, concat_axis=0, tiled=True)]
    all_to_all x3 -> x0, starting transfers between devices: 16.9 us -> none  [the longest x1 7.41 us: per_device(): lax.all_to_all(segment_out, 'seq', split_axis=0, concat_axis=0, tiled=True)]
    unnamed x1 -> x0, blocking collectives: 12.4 us -> none
    gather x6 -> x0, local copies, waits for them, and re-layouts: 3.6 us -> none  [the longest x1 1.43 us: per_device(): jnp.take(segment, bucket_index, axis=0, mode='fill', fill_value=-1)]
    reduce_sum x6 -> x0, other arithmetic: 2.32 us -> none  [the longest x1 0.87 us: per_device(): text_limit = jnp.sum(seg_hot * text_count[None, :], axis=1)]
    select_n x5 -> x0, other arithmetic: 1.89 us -> none  [the longest x2 1.1 us: per_device(): jnp.take(stacked, bucket_index, axis=1, mode='fill', fill_value=0)]
    convert_element_type x7 -> x0, other arithmetic: 1.87 us -> none  [the longest x1 0.82 us: per_device(): return mixed.astype(jnp.bfloat16)]
  transfers between devices with their start and end apart: 3 -> 0, of which waited for: 2 -> 0; matrix products, arithmetic and copies ran while one was open for 14% -> 0% of each run, Pallas kernels for 0% -> 0%
where the time goes in v1:
time: 33.6 us; the launch traced here: 33.4 us
  Pallas kernels  31.8 us (95%)
  local copies, waits for them, and re-layouts  1.62 us (5%)
    pallas_call x1, Pallas kernels, fused(): pl.pallas_call(functools.partial(fused_kernel, devices, text_count.shape[...  31.8 us
    unnamed x1, local copies, waits for them, and re-layouts  1.62 us

profile of v1, /device:TPU:0, one launch (start us, length us, event | category | flops | bytes accessed | tf_op | source)
XLA Modules:
  0.0 33.4 jit_solution(7056449600117107362)
XLA Ops:
  0.0 31.8 %shard_map.91 = bf16[32,3072]{1,0:T(8,128)(2,1)} custom-call(s32[4]{0:T(128)} %text_ref.1, s32[1,32]{1,0:T(1,128)} %bitcast.1, bf16[32,3072]{1,0:T(8,128)(2,1)} %hidden_ref.1, bf16[32,3072]{1,0:T(8,128)(2,1)} %query_hbm.1, bf16[32,3072]{1,0:T(8,128)(2,1)} %key_hbm.1, bf16[32,3072]{1,0:T(8,128)(2,1)} %value_hbm.1, f32[2,128]{1,0:T(2,128)} %query_gain_ref.1, ...), custom_call_target="tpu_custom_call" | custom-call | tf_op jit(solution)/shard_map/pallas_call | solution.py:347
  31.8 1.6 %copy.11 = bf16[32,3072]{1,0:T(8,128)(2,1)} copy(bf16[32,3072]{1,0:T(8,128)(2,1)} %shard_map.91) | data formatting | bytes 393216

commit v2 on v1

--- a/solution.py
+++ b/solution.py
@@ -132,15 +132,16 @@
 
 
 def fused_kernel(
-    devices, requests, text_ref, segment_ref, hidden_ref, query_hbm, key_hbm, value_hbm,
-    query_gain_ref, key_gain_ref, gate_ref, out_ref,
+    devices, requests, segment_hbm, query_hbm, key_hbm, value_hbm,
+    text_hbm, hidden_hbm, query_gain_hbm, key_gain_hbm, gate_hbm, out_hbm,
+    text_ref, hidden_ref, query_gain_ref, key_gain_ref, gate_ref, out_ref,
     stage, recv, query_n, key_n, result, back, seg_all, hot, text, bias, gate_rows,
-    stage_sem, own_sem, seg_own_sem, seg_send, seg_recv,
+    stage_sem, own_sem, seg_own_sem, load_sem, store_sem, seg_send, seg_recv,
     out_send, out_recv, relay_send, relay_recv, back_send, back_recv,
 ):
     chips = devices // 2
-    tok = hidden_ref.shape[0]
-    per_chip = hidden_ref.shape[1] // HEAD_DIM // chips
+    tok = hidden_hbm.shape[0]
+    per_chip = hidden_hbm.shape[1] // HEAD_DIM // chips
     tokens = devices * tok
     mine = chips * tok
     me = lax.axis_index("seq")
@@ -158,11 +159,13 @@
         )
 
     barrier = pltpu.get_barrier_semaphore()
-    for step in range(1, devices):
+    for device in [(chip + step) % chips * 2 + core for step in range(1, chips)] + [partner]:
         pl.semaphore_signal(
-            barrier, inc=1, device_id={"seq": (me + step) % devices},
+            barrier, inc=1, device_id={"seq": device},
             device_id_type=pl.DeviceIdType.MESH,
         )
+    seg_own = pltpu.make_async_copy(segment_hbm, seg_all.at[me], seg_own_sem)
+    seg_own.start()
     for head in range(per_chip):
         for step in range(1, chips):
             target = (chip + step) % chips
@@ -178,30 +181,46 @@
                 recv.at[head, me, part],
                 own_sem.at[head],
             ).start()
-    seg_own = pltpu.make_async_copy(segment_ref, seg_all.at[me], seg_own_sem)
-    seg_own.start()
-    pl.semaphore_wait(barrier, devices - 1)
+    loads = [
+        pltpu.make_async_copy(source, target, load_sem.at[place])
+        for place, (source, target) in enumerate(
+            (
+                (text_hbm, text_ref), (query_gain_hbm, query_gain_ref),
+                (key_gain_hbm, key_gain_ref), (gate_hbm, gate_ref), (hidden_hbm, hidden_ref),
+            )
+        )
+    ]
+    for copy in loads:
+        copy.start()
+    seg_own.wait()
+    pl.semaphore_wait(barrier, chips)
 
     seg_copies = []
-    for step in range(1, devices):
+    seg_relays = []
+
+    def send_ids(source, kind, step, device):
         copy = remote(
-            segment_ref, seg_all.at[me], seg_send.at[step - 1], seg_recv.at[step - 1],
-            (me + step) % devices,
+            seg_all.at[source], seg_all.at[source],
+            seg_send.at[kind, step], seg_recv.at[kind, step], device,
         )
         copy.start()
-        seg_copies.append(copy)
+        return copy
+
+    for step in range(chips - 1, 0, -1):
+        seg_copies.insert(0, send_ids(me, 0, step, (chip + step) % chips * 2 + core))
+    seg_relays.append(send_ids(me, 1, 0, partner))
     out_copies = []
     for head in range(per_chip):
         pltpu.make_async_copy(stage.at[head], stage.at[head], stage_sem.at[head]).wait()
         row = []
-        for step in range(1, chips):
+        for step in range(chips - 1, 0, -1):
             copy = remote(
                 stage.at[head, step - 1], recv.at[head, me],
                 out_send.at[head, step - 1], out_recv.at[head, step - 1],
                 (chip + step) % chips * 2 + core,
             )
             copy.start()
-            row.append(copy)
+            row.insert(0, copy)
         out_copies.append(row)
 
     relay_copies = []
@@ -220,9 +239,14 @@
         ).wait()
         relay_copies.append([relay(head, 0, me)])
 
-    seg_own.wait()
-    for copy in seg_copies:
+    for step in range(1, chips):
+        seg_copies[step - 1].wait_recv()
+        source = (chip + chips - step) % chips * 2 + core
+        seg_relays.append(send_ids(source, 1, step, partner))
+    for copy in seg_relays:
         copy.wait_recv()
+    for copy in loads:
+        copy.wait()
     eye = (
         lax.broadcasted_iota(jnp.int32, (tok, tok), 0)
         == lax.broadcasted_iota(jnp.int32, (tok, tok), 1)
@@ -242,7 +266,7 @@
     lane = lax.broadcasted_iota(jnp.int32, (1, LANES), 1)
     limit = jnp.zeros((1, LANES), jnp.int32)
     for r in range(requests):
-        limit = jnp.where(lane == r, text_ref[r], limit)
+        limit = jnp.where(lane == r, text_ref[0:1, r : r + 1], limit)
     inside = jnp.where(before < limit.astype(jnp.float32), all_hot.astype(jnp.float32), 0.0)
     ones = jnp.ones((LANES, LANES), jnp.bfloat16)
     text[...] = jnp.dot(
@@ -317,6 +341,9 @@
             hidden_ref[:, columns(index)].astype(jnp.float32)
             + gate_rows[index] * attention.astype(jnp.float32)
         ).astype(jnp.bfloat16)
+        pltpu.make_async_copy(
+            out_ref.at[:, columns(index)], out_hbm.at[:, columns(index)], store_sem
+        ).start()
 
     for head in range(per_chip):
         finish(chip * per_chip + head, result[head, chip])
@@ -324,12 +351,13 @@
             back_copies[head][step - 1].wait_recv()
             index = (chip + chips - step) % chips * per_chip + head
             finish(index, back[index])
-    for copy in seg_copies:
+    for copy in seg_copies + seg_relays:
         copy.wait_send()
     for rows in (out_copies, relay_copies, back_copies):
         for row in rows:
             for copy in row:
                 copy.wait_send()
+    pltpu.make_async_copy(out_ref, out_hbm, store_sem).wait()
 
 
 def fused(
@@ -340,17 +368,21 @@
     tok, width = hidden.shape
     heads = width // HEAD_DIM
     per_chip = heads // chips
-    vmem = pl.BlockSpec(memory_space=pltpu.VMEM)
     hbm = pl.BlockSpec(memory_space=pl.ANY)
     block = (tok, HEAD_DIM)
     dma = pltpu.SemaphoreType.DMA
     return pl.pallas_call(
         functools.partial(fused_kernel, devices, text_count.shape[0]),
         out_shape=jax.ShapeDtypeStruct((tok, width), jnp.bfloat16),
-        in_specs=[pl.BlockSpec(memory_space=pltpu.SMEM), vmem, vmem, hbm, hbm, hbm]
-        + [vmem] * 3,
-        out_specs=vmem,
+        in_specs=[hbm] * 9,
+        out_specs=hbm,
         scratch_shapes=[
+            pltpu.VMEM((1, text_count.shape[0]), jnp.int32),
+            pltpu.VMEM(hidden.shape, hidden.dtype),
+            pltpu.VMEM(query_gain.shape, query_gain.dtype),
+            pltpu.VMEM(key_gain.shape, key_gain.dtype),
+            pltpu.VMEM(gate_table.shape, gate_table.dtype),
+            pltpu.VMEM(hidden.shape, jnp.bfloat16),
             pltpu.VMEM((per_chip, chips - 1, 3) + block, jnp.bfloat16),
             pltpu.VMEM((per_chip, devices, 3) + block, jnp.bfloat16),
             pltpu.VMEM((chips,) + block, jnp.bfloat16),
@@ -365,8 +397,10 @@
             dma((per_chip,)),
             dma((per_chip,)),
             dma,
-            dma((devices - 1,)),
-            dma((devices - 1,)),
+            dma((5,)),
+            dma,
+            dma((2, chips)),
+            dma((2, chips)),
             dma((per_chip, chips - 1)),
             dma((per_chip, chips - 1)),
             dma((per_chip, chips)),
@@ -376,8 +410,8 @@
         ],
         compiler_params=pltpu.CompilerParams(collective_id=0, has_side_effects=True),
     )(
-        text_count, segment.reshape(1, tok), hidden, queries, key_rows, values,
-        query_gain, key_gain, gate_table,
+        segment.reshape(1, tok), queries, key_rows, values,
+        text_count.reshape(1, -1), hidden, query_gain, key_gain, gate_table,
     )
 
 

time: 33.6 us -> 30.8 us (0.917)
  Pallas kernels: 31.8 us -> 29 us
    pallas_call x1, Pallas kernels: 31.8 us -> 29 us  [fused(): pl.pallas_call(functools.partial(fused_kernel, devices, text_count.shape[...]
where the time goes in v2:
time: 30.8 us; the launch traced here: 30.6 us
  Pallas kernels  29 us (94%)
  local copies, waits for them, and re-layouts  1.62 us (5%)
    pallas_call x1, Pallas kernels, fused(): pl.pallas_call(functools.partial(fused_kernel, devices, text_count.shape[...  29 us
    unnamed x1, local copies, waits for them, and re-layouts  1.62 us

profile of v2, /device:TPU:0, one launch (start us, length us, event | category | flops | bytes accessed | tf_op | source)
XLA Modules:
  0.0 30.6 jit_solution(12232211894047056378)
XLA Ops:
  0.0 29.0 %shard_map.91 = bf16[32,3072]{1,0:T(8,128)(2,1)} custom-call(s32[1,32]{1,0:T(1,128)} %bitcast.2, bf16[32,3072]{1,0:T(8,128)(2,1)} %query_hbm.1, bf16[32,3072]{1,0:T(8,128)(2,1)} %key_hbm.1, bf16[32,3072]{1,0:T(8,128)(2,1)} %value_hbm.1, s32[1,4]{1,0:T(1,128)} %bitcast.3, bf16[32,3072]{1,0:T(8,128)(2,1)} %hidden_hbm.1, f32[2,128]{1,0:T(2,128)} %query_gain_hbm.1, ...), custom_call_target="tpu_custom_call" | custom-call | tf_op jit(solution)/shard_map/pallas_call | solution.py:374
  29.0 1.6 %copy.11 = bf16[32,3072]{1,0:T(8,128)(2,1)} copy(bf16[32,3072]{1,0:T(8,128)(2,1)} %shard_map.91) | data formatting | bytes 393216

commit v3 on v2

--- a/solution.py
+++ b/solution.py
@@ -149,6 +149,9 @@
     partner = me + 1 - 2 * core
     sources = (query_hbm, key_hbm, value_hbm)
 
+    def offset(step, of_core):
+        return step + of_core * (chips - 2 * step)
+
     def columns(head):
         return pl.ds(pl.multiple_of(head * HEAD_DIM, HEAD_DIM), HEAD_DIM)
 
@@ -159,7 +162,7 @@
         )
 
     barrier = pltpu.get_barrier_semaphore()
-    for device in [(chip + step) % chips * 2 + core for step in range(1, chips)] + [partner]:
+    for device in [(chip + offset(step, core)) % chips * 2 + core for step in range(1, chips)] + [partner]:
         pl.semaphore_signal(
             barrier, inc=1, device_id={"seq": device},
             device_id_type=pl.DeviceIdType.MESH,
@@ -168,7 +171,7 @@
     seg_own.start()
     for head in range(per_chip):
         for step in range(1, chips):
-            target = (chip + step) % chips
+            target = (chip + offset(step, core)) % chips
             for part, source in enumerate(sources):
                 pltpu.make_async_copy(
                     source.at[:, columns(target * per_chip + head)],
@@ -207,7 +210,7 @@
         return copy
 
     for step in range(chips - 1, 0, -1):
-        seg_copies.insert(0, send_ids(me, 0, step, (chip + step) % chips * 2 + core))
+        seg_copies.insert(0, send_ids(me, 0, step, (chip + offset(step, core)) % chips * 2 + core))
     seg_relays.append(send_ids(me, 1, 0, partner))
     out_copies = []
     for head in range(per_chip):
@@ -217,7 +220,7 @@
             copy = remote(
                 stage.at[head, step - 1], recv.at[head, me],
                 out_send.at[head, step - 1], out_recv.at[head, step - 1],
-                (chip + step) % chips * 2 + core,
+                (chip + offset(step, core)) % chips * 2 + core,
             )
             copy.start()
             row.insert(0, copy)
@@ -241,7 +244,7 @@
 
     for step in range(1, chips):
         seg_copies[step - 1].wait_recv()
-        source = (chip + chips - step) % chips * 2 + core
+        source = (chip + chips - offset(step, core)) % chips * 2 + core
         seg_relays.append(send_ids(source, 1, step, partner))
     for copy in seg_relays:
         copy.wait_recv()
@@ -302,7 +305,7 @@
     for head in range(per_chip):
         for step in range(1, chips):
             out_copies[head][step - 1].wait_recv()
-            source = (chip + chips - step) % chips * 2 + core
+            source = (chip + chips - offset(step, core)) % chips * 2 + core
             relay_copies[head].append(relay(head, step, source))
         for c in range(chips):
             n = 2 * c + core
@@ -310,7 +313,7 @@
             key_n[n] = normed(recv[head, n, 1], gain_of(key_gain, n))
         for step in range(chips):
             relay_copies[head][step].wait_recv()
-            n = (chip + chips - step) % chips * 2 + 1 - core
+            n = (chip + chips - offset(step, 1 - core)) % chips * 2 + 1 - core
             key_n[n] = normed(recv[head, n, 1], gain_of(key_gain, n))
         keys = key_n[...].reshape(tokens, HEAD_DIM)
         vals = recv[head, :, 2].reshape(tokens, HEAD_DIM)
@@ -326,7 +329,7 @@
         ).astype(jnp.bfloat16).reshape(chips, tok, HEAD_DIM)
         row = []
         for step in range(1, chips):
-            target = (chip + step) % chips
+            target = (chip + offset(step, core)) % chips
             copy = remote(
                 result.at[head, target], back.at[chip * per_chip + head],
                 back_send.at[head, step - 1], back_recv.at[head, step - 1],
@@ -349,7 +352,7 @@
         finish(chip * per_chip + head, result[head, chip])
         for step in range(1, chips):
             back_copies[head][step - 1].wait_recv()
-            index = (chip + chips - step) % chips * per_chip + head
+            index = (chip + chips - offset(step, core)) % chips * per_chip + head
             finish(index, back[index])
     for copy in seg_copies + seg_relays:
         copy.wait_send()

time: 30.8 us -> 31.3 us (1.016)
  Pallas kernels: 29 us -> 29.5 us
    pallas_call x1, Pallas kernels: 29 us -> 29.5 us  [fused(): pl.pallas_call(functools.partial(fused_kernel, devices, text_count.shape[...]
where the time goes in v3:
time: 31.3 us; the launch traced here: 31.1 us
  Pallas kernels  29.5 us (94%)
  local copies, waits for them, and re-layouts  1.62 us (5%)
    pallas_call x1, Pallas kernels, fused(): pl.pallas_call(functools.partial(fused_kernel, devices, text_count.shape[...  29.5 us
    unnamed x1, local copies, waits for them, and re-layouts  1.62 us

profile of v3, /device:TPU:0, one launch (start us, length us, event | category | flops | bytes accessed | tf_op | source)
XLA Modules:
  0.0 31.1 jit_solution(12516205002544513257)
XLA Ops:
  0.0 29.5 %shard_map.91 = bf16[32,3072]{1,0:T(8,128)(2,1)} custom-call(s32[1,32]{1,0:T(1,128)} %bitcast.2, bf16[32,3072]{1,0:T(8,128)(2,1)} %query_hbm.1, bf16[32,3072]{1,0:T(8,128)(2,1)} %key_hbm.1, bf16[32,3072]{1,0:T(8,128)(2,1)} %value_hbm.1, s32[1,4]{1,0:T(1,128)} %bitcast.3, bf16[32,3072]{1,0:T(8,128)(2,1)} %hidden_hbm.1, f32[2,128]{1,0:T(2,128)} %query_gain_hbm.1, ...), custom_call_target="tpu_custom_call" | custom-call | tf_op jit(solution)/shard_map/pallas_call | solution.py:377
  29.5 1.6 %copy.11 = bf16[32,3072]{1,0:T(8,128)(2,1)} copy(bf16[32,3072]{1,0:T(8,128)(2,1)} %shard_map.91) | data formatting | bytes 393216
